TPU v7x, 32 devices: a whole 2x2x4 slice. The times are simulated.
32 devices in a mesh: ga: 2 (over y), gx: 4 (over z), gy: 2 (over x), gz: 2 (over core).
Axes of the slice: x: 2, y: 2, z: 4, core: 2. Of those that a mesh axis runs over, the one named last changes fastest.
Arguments:
- state: bfloat16 [8, 256, 4, 512], P(('ga', 'gx'), None, None, 'gy'), parts along dimension 0, may hold values from -6 to 6
- left_env: bfloat16 [16, 8, 256, 256], P(None, ('ga', 'gx')), parts along dimension 1, may hold values from -0.375 to 0.375
- mpo_terms: bfloat16 [16, 16, 4, 4], P(None, 'gz'), may hold values from -0.75 to 0.75
- right_env: bfloat16 [16, 1024, 256], P('gz', ('ga', 'gy')), parts along dimension 1, may hold values from -0.09375 to 0.09375
- term_charge: int32 [16], replicated, may hold values from 0 to 2, as said below
- charge_order: int32 [8], P('ga'), parts along dimension 0, may hold values from 0 to 3, as said below
- sector_dims: int32 [8], P('ga'), parts along dimension 0, may hold values from 128 to 256
Outputs:
- result_state: bfloat16 [8, 256, 4, 512], P(('ga', 'gx'), None, 'gz', 'gy'), parts along dimension 0
There are 2 independent parts, one for each index of `ga`. A program takes and returns all parts, laid end to end along the dimension named above; an argument that names none is the same for every part. Nothing has to cross between parts.
Inputs may be any that keep to these rules, and one draw needn't show every extreme that they name: `charge_order`: each value appears once. `term_charge`: each of 0, 1 and 2 appears at least once.
All inputs are finite; a program needn't handle non-finite values.
Results may differ from a plain program's by a relative error of at most 0.0057.
Values may be sent and summed in bfloat16 or wider, within the bound.
A program may use at most 64 MiB of HBM per device.

v0:
```python
import jax
import jax.numpy as jnp
from jax import lax
from jax.sharding import PartitionSpec as P


def source_table(charge_order, first_sector, sector_count):
    own_charge = lax.dynamic_slice_in_dim(charge_order, first_sector, sector_count, 0)
    wanted = own_charge[:, None] + jnp.arange(3, dtype=jnp.int32)[None, :] - 1
    matches = charge_order[None, None, :] == wanted[:, :, None]
    sector_ids = jnp.arange(charge_order.shape[0], dtype=jnp.int32)
    found_ids = jnp.sum(jnp.where(matches, sector_ids[None, None, :], 0), axis=2)
    return jnp.where(jnp.any(matches, axis=2), found_ids, -1)


def make_picker(sources):

    def picker(carry, piece, start):
        piece_count = piece.shape[0]
        piece_ids = jnp.arange(piece_count, dtype=jnp.int32)
        selector = (sources[:, :, None] == piece_ids[None, None, :]).astype(jnp.bfloat16)
        taken = jnp.einsum("jck,kxpb->jcxpb", selector, piece, preferred_element_type=jnp.float32)
        return taken.astype(jnp.bfloat16)

    return picker


def apply_left(environment, charges, picked):

    def one_term(pair_item):
        matrix, charge_shift = pair_item
        source_block = lax.dynamic_index_in_dim(picked, charge_shift, 1, keepdims=False)
        product = jnp.einsum(
            "jxa,japb->jxpb", matrix, source_block, preferred_element_type=jnp.float32
        )
        return product.astype(jnp.bfloat16)

    return lax.map(one_term, (environment, charges))


def body(state, left_env, mpo_terms, right_env, term_charge, charge_order, sector_dims):
    sectors = state.shape[0]
    row_count = state.shape[1]
    first_sector = lax.axis_index("gx") * sectors
    sources = source_table(charge_order, first_sector, sectors)
    picker = make_picker(sources)
    blank_carry = jnp.zeros((sectors, 3) + state.shape[1:], jnp.bfloat16)
    picked = picker(blank_carry, lax.all_gather(state, "gx", axis=0, tiled=True), jnp.int32(0))
    term_share = left_env.shape[0] // lax.axis_size("gz")
    first_term = lax.axis_index("gz") * term_share
    env_part = lax.dynamic_slice_in_dim(left_env, first_term, term_share, 0)
    charge_part = lax.dynamic_slice_in_dim(term_charge, first_term, term_share, 0)
    own_terms = apply_left(env_part, charge_part, picked)
    applied = lax.all_gather(own_terms, "gz", axis=0, tiled=True)
    mixed_terms = jnp.einsum(
        "uvpq,ujxqb->vjxpb", mpo_terms, applied, preferred_element_type=jnp.float32
    ).astype(jnp.bfloat16)
    partial_out = jnp.einsum(
        "vjxpb,vbc->jxpc", mixed_terms, right_env, preferred_element_type=jnp.float32
    )
    own_dims = lax.dynamic_slice_in_dim(sector_dims, first_sector, sectors, 0)
    row_mask = (jnp.arange(row_count, dtype=jnp.int32)[None, :] < own_dims[:, None]).astype(
        jnp.float32
    )
    partial_out = partial_out * row_mask[:, :, None, None]
    summed = lax.psum_scatter(partial_out, "gz", scatter_dimension=2, tiled=True)
    return summed.astype(jnp.bfloat16)


def solution(mesh):
    return jax.shard_map(
        body,
        mesh=mesh,
        in_specs=(
            P(("ga", "gx"), None, None, "gy"),
            P(None, ("ga", "gx"), None, None),
            P(None, "gz", None, None),
            P("gz", ("ga", "gy"), None),
            P(),
            P("ga"),
            P("ga"),
        ),
        out_specs=P(("ga", "gx"), None, "gz", "gy"),
        check_vma=False,
    )
```

profile of v0, /device:TPU:1, one launch (start us, length us, event | category | flops | bytes accessed | tf_op | source)
XLA Modules:
  0.0 154.8 jit_solution(4752129319796070379)
XLA Ops:
  6.5 2.1 %copy.22 = bf16[1,256,4,256]{3,1,2,0:T(8,128)(2,1)} copy(bf16[1,256,4,256]{3,2,1,0:T(4,128)(2,1)} %param.9) | data formatting | bytes 1048576 | tf_op args[0]
  8.7 1.3 dynamic_slice.26
  10.0 0.7 dynamic_slice.25
  10.7 0.7 add_add_fusion
  11.4 0.9 compare_reduce_fusion
  12.3 0.9 fusion.32
  13.3 43.2 %all-gather.3.cloned.1.call-done = bf16[4,256,4,256]{3,1,2,0:T(8,128)(2,1)} async-done(((bf16[1,256,4,256]{3,1,2,0:T(8,128)(2,1)}), bf16[4,256,4,256]{3,1,2,0:T(8,128)(2,1)}) %all-gather.3.cloned.1.call-update) | async-done | bytes 2097168 | tf_op jit(solution)/shard_map/all_gather | solution.py:48
  56.5 3.4 %convert_bitcast_fusion = bf16[1,3,256,4,256]{4,1,3,2,0:T(4,128)(2,1)S(1)} fusion(bf16[4,256,4,256]{3,1,2,0:T(8,128)(2,1)} %all-gather.3.cloned.1.call-done, s32[3]{0:T(128)S(1)} %broadcast_select_fusion), kind=kOutput, calls=%fused_computation.16 | convolution fusion | flops 7077900 | bytes 3670028 | tf_op jit(solution)/shard_map/jck,kxpb->jcxpb/dot_general | solution.py:22
  59.9 1.9 %copy.24 = bf16[1,3,256,4,256]{4,2,3,1,0:T(8,128)(2,1)} copy(bf16[1,3,256,4,256]{4,1,3,2,0:T(4,128)(2,1)S(1)} %convert_bitcast_fusion) | data formatting | bytes 3145728 | tf_op jit(solution)/shard_map/while | solution.py:38
  61.7 39.0 %while.10 = (s32[]{:T(128)}, bf16[8,1,256,4,256]{4,2,3,1,0:T(8,128)(2,1)}, bf16[8,1,256,256]{3,2,1,0:T(8,128)(2,1)S(1)}, s32[8]{0:T(128)S(1)}, bf16[1,3,256,4,25...) while((s32[]{:T(128)}, bf16[8,1,256,4,256]{4,2,3,1,0:T(8,128)(2,1)}, ...), condition=%wide.region_3.4_spmd, body=%wide.region_2.3_spmd.sunk | while | flops 134479872 | bytes 1180807 | solution.py:38
  61.7 0.7 dynamic_slice.42
  64.4 2.1 %fusion.39 = bf16[8,1,256,4,256]{4,2,3,1,0:T(8,128)(2,1)} fusion(bf16[8,1,256,4,256]{4,2,3,1,0:T(8,128)(2,1)} %get-tuple-element.98, s32[]{:T(128)} %get-tuple-element.97, bf16[1,3,256,4,256]{4,2,3,1,0:T(8,128)(2,1)} %get-tuple-element.109, s32[]{:T(128)S(6)} %select_n.43, bf16[8,1,256,256]{3,2,1,0:T(8,128)(2,1)S(1)} %get-tuple-element.107), kind=kOutput, calls=%fused_computation.2.clone.1 | convolution fusion | flops 134479872 | bytes 1180676 | tf_op jit(solution)/shard_map/while/body/eval_jaxpr/jxa,japb->jxpb/dot_general | solution.py:33
  66.6 0.7 dynamic_slice.42
  69.3 2.1 %fusion.39 = bf16[8,1,256,4,256]{4,2,3,1,0:T(8,128)(2,1)} fusion(bf16[8,1,256,4,256]{4,2,3,1,0:T(8,128)(2,1)} %get-tuple-element.98, s32[]{:T(128)} %get-tuple-element.97, bf16[1,3,256,4,256]{4,2,3,1,0:T(8,128)(2,1)} %get-tuple-element.109, s32[]{:T(128)S(6)} %select_n.43, bf16[8,1,256,256]{3,2,1,0:T(8,128)(2,1)S(1)} %get-tuple-element.107), kind=kOutput, calls=%fused_computation.2.clone.1 | convolution fusion | flops 134479872 | bytes 1180676 | tf_op jit(solution)/shard_map/while/body/eval_jaxpr/jxa,japb->jxpb/dot_general | solution.py:33
  71.5 0.7 dynamic_slice.42
  74.2 2.2 %fusion.39 = bf16[8,1,256,4,256]{4,2,3,1,0:T(8,128)(2,1)} fusion(bf16[8,1,256,4,256]{4,2,3,1,0:T(8,128)(2,1)} %get-tuple-element.98, s32[]{:T(128)} %get-tuple-element.97, bf16[1,3,256,4,256]{4,2,3,1,0:T(8,128)(2,1)} %get-tuple-element.109, s32[]{:T(128)S(6)} %select_n.43, bf16[8,1,256,256]{3,2,1,0:T(8,128)(2,1)S(1)} %get-tuple-element.107), kind=kOutput, calls=%fused_computation.2.clone.1 | convolution fusion | flops 134479872 | bytes 1180676 | tf_op jit(solution)/shard_map/while/body/eval_jaxpr/jxa,japb->jxpb/dot_general | solution.py:33
  76.3 0.7 dynamic_slice.42
  79.1 2.1 %fusion.39 = bf16[8,1,256,4,256]{4,2,3,1,0:T(8,128)(2,1)} fusion(bf16[8,1,256,4,256]{4,2,3,1,0:T(8,128)(2,1)} %get-tuple-element.98, s32[]{:T(128)} %get-tuple-element.97, bf16[1,3,256,4,256]{4,2,3,1,0:T(8,128)(2,1)} %get-tuple-element.109, s32[]{:T(128)S(6)} %select_n.43, bf16[8,1,256,256]{3,2,1,0:T(8,128)(2,1)S(1)} %get-tuple-element.107), kind=kOutput, calls=%fused_computation.2.clone.1 | convolution fusion | flops 134479872 | bytes 1180676 | tf_op jit(solution)/shard_map/while/body/eval_jaxpr/jxa,japb->jxpb/dot_general | solution.py:33
  81.2 0.7 dynamic_slice.42
  83.9 2.1 %fusion.39 = bf16[8,1,256,4,256]{4,2,3,1,0:T(8,128)(2,1)} fusion(bf16[8,1,256,4,256]{4,2,3,1,0:T(8,128)(2,1)} %get-tuple-element.98, s32[]{:T(128)} %get-tuple-element.97, bf16[1,3,256,4,256]{4,2,3,1,0:T(8,128)(2,1)} %get-tuple-element.109, s32[]{:T(128)S(6)} %select_n.43, bf16[8,1,256,256]{3,2,1,0:T(8,128)(2,1)S(1)} %get-tuple-element.107), kind=kOutput, calls=%fused_computation.2.clone.1 | convolution fusion | flops 134479872 | bytes 1180676 | tf_op jit(solution)/shard_map/while/body/eval_jaxpr/jxa,japb->jxpb/dot_general | solution.py:33
  86.1 0.7 dynamic_slice.42
  88.8 2.2 %fusion.39 = bf16[8,1,256,4,256]{4,2,3,1,0:T(8,128)(2,1)} fusion(bf16[8,1,256,4,256]{4,2,3,1,0:T(8,128)(2,1)} %get-tuple-element.98, s32[]{:T(128)} %get-tuple-element.97, bf16[1,3,256,4,256]{4,2,3,1,0:T(8,128)(2,1)} %get-tuple-element.109, s32[]{:T(128)S(6)} %select_n.43, bf16[8,1,256,256]{3,2,1,0:T(8,128)(2,1)S(1)} %get-tuple-element.107), kind=kOutput, calls=%fused_computation.2.clone.1 | convolution fusion | flops 134479872 | bytes 1180676 | tf_op jit(solution)/shard_map/while/body/eval_jaxpr/jxa,japb->jxpb/dot_general | solution.py:33
  93.7 2.1 %fusion.39 = bf16[8,1,256,4,256]{4,2,3,1,0:T(8,128)(2,1)} fusion(bf16[8,1,256,4,256]{4,2,3,1,0:T(8,128)(2,1)} %get-tuple-element.98, s32[]{:T(128)} %get-tuple-element.97, bf16[1,3,256,4,256]{4,2,3,1,0:T(8,128)(2,1)} %get-tuple-element.109, s32[]{:T(128)S(6)} %select_n.43, bf16[8,1,256,256]{3,2,1,0:T(8,128)(2,1)S(1)} %get-tuple-element.107), kind=kOutput, calls=%fused_computation.2.clone.1 | convolution fusion | flops 134479872 | bytes 1180676 | tf_op jit(solution)/shard_map/while/body/eval_jaxpr/jxa,japb->jxpb/dot_general | solution.py:33
  95.8 0.7 dynamic_slice.42
  98.6 2.2 %fusion.39 = bf16[8,1,256,4,256]{4,2,3,1,0:T(8,128)(2,1)} fusion(bf16[8,1,256,4,256]{4,2,3,1,0:T(8,128)(2,1)} %get-tuple-element.98, s32[]{:T(128)} %get-tuple-element.97, bf16[1,3,256,4,256]{4,2,3,1,0:T(8,128)(2,1)} %get-tuple-element.109, s32[]{:T(128)S(6)} %select_n.43, bf16[8,1,256,256]{3,2,1,0:T(8,128)(2,1)S(1)} %get-tuple-element.107), kind=kOutput, calls=%fused_computation.2.clone.1 | convolution fusion | flops 134479872 | bytes 1180676 | tf_op jit(solution)/shard_map/while/body/eval_jaxpr/jxa,japb->jxpb/dot_general | solution.py:33
  100.7 6.5 %copy.25 = bf16[8,1,256,4,256]{4,0,3,2,1:T(8,128)(2,1)} copy(bf16[8,1,256,4,256]{4,2,3,1,0:T(8,128)(2,1)} %get-tuple-element.32) | data formatting | bytes 8388608 | tf_op jit(solution)/shard_map/while | solution.py:38
  109.1 15.7 %all-gather.5.cloned.1.call-done = bf16[16,1,256,4,256]{4,0,3,2,1:T(8,128)(2,1)} async-done(((bf16[8,1,256,4,256]{4,0,3,2,1:T(8,128)(2,1)}), bf16[16,1,256,4,256]{4,0,3,2,1:T(8,128)(2,1)}) %all-gather.5.cloned.1.call-update) | async-done | bytes 8388624 | tf_op jit(solution)/shard_map/all_gather | solution.py:54
  124.9 5.9 %fusion.9 = bf16[8,256,4,256]{3,0,2,1:T(8,128)(2,1)S(1)} fusion(bf16[16,1,256,4,256]{4,0,3,2,1:T(8,128)(2,1)} %all-gather.5.cloned.1.call-done, bf16[16,8,4,4]{0,3,2,1:T(4,128)(2,1)S(1)} %copy-done.2), kind=kOutput, calls=%fused_computation.11 | convolution fusion | flops 270532608 | bytes 12587008 | tf_op jit(solution)/shard_map/uvpq,ujxqb->vjxpb/dot_general | solution.py:55
  130.9 5.6 %fusion.24 = f32[1,256,4,256]{3,1,2,0:T(8,128)} fusion(bf16[8,256,4,256]{3,0,2,1:T(8,128)(2,1)S(1)} %fusion.9, bf16[8,256,256]{2,1,0:T(8,128)(2,1)S(1)} %copy-done.1, f32[256]{0:T(256)S(1)} %compare_convert_fusion), kind=kOutput, calls=%fused_computation.19 | convolution fusion | flops 1074003968 | bytes 6292480 | tf_op jit(solution)/shard_map/vjxpb,vbc->jxpc/dot_general | solution.py:58
  136.5 9.8 %reduce-scatter.2.cloned.1.call-done = f32[1,256,2,256]{3,1,2,0:T(8,128)} async-done(((f32[1,256,4,256]{3,1,2,0:T(8,128)}), f32[1,256,2,256]{3,1,2,0:T(8,128)}) %reduce-scatter.2.cloned.1.call-update) | async-done | bytes 524304 | tf_op jit(solution)/shard_map/reduce_scatter | solution.py:66
  146.2 1.1 convert_element_type.38
  147.3 1.0 copy.28
  (20 shorter events, 2.7 us)
Async XLA Ops:
  6.5 6.7 %copy-start = (bf16[16,1,256,256]{3,2,1,0:T(8,128)(2,1)S(1)}, bf16[16,1,256,256]{3,2,1,0:T(8,128)(2,1)}, u32[]{:S(2)}) copy-start(bf16[16,1,256,256]{3,2,1,0:T(8,128)(2,1)} %param.10) | copy-start | bytes 6291460
  6.5 50.0 %all-gather.3.cloned.1.call-start = ((), (), s32[]{:S(2)}) async-start(), calls=%async_computation.1 | async-start | bytes 2621440 | tf_op jit(solution)/shard_map/all_gather | solution.py:48
  8.6 116.3 %all-gather.5.cloned.1.call-start = ((), (), s32[]{:S(2)}) async-start(), calls=%async_computation.2 | async-start | bytes 12582912 | tf_op jit(solution)/shard_map/all_gather | solution.py:54
  107.2 0.7 copy-start.3
  107.2 17.7 %copy-start.2 = (bf16[16,8,4,4]{0,3,2,1:T(4,128)(2,1)S(1)}, bf16[16,8,4,4]{0,3,2,1:T(4,128)(2,1)}, u32[]{:S(2)}) copy-start(bf16[16,8,4,4]{0,3,2,1:T(4,128)(2,1)} %param.11) | copy-start | bytes 12292
  107.3 38.9 %reduce-scatter.2.cloned.1.call-start = ((), (), s32[]{:S(2)}) async-start(), calls=%async_computation.3 | async-start | bytes 1572864 | tf_op jit(solution)/shard_map/reduce_scatter | solution.py:66
  109.1 21.7 %copy-start.1 = (bf16[8,256,256]{2,1,0:T(8,128)(2,1)S(1)}, bf16[8,256,256]{2,1,0:T(8,128)(2,1)}, u32[]{:S(2)}) copy-start(bf16[8,256,256]{2,1,0:T(8,128)(2,1)} %param.12) | copy-start | bytes 3145732
Sparse Core Ops, SparseCore 0:
  8.9 47.5 all-gather.2
  107.4 17.4 all-gather.4
  136.6 9.5 reduce-scatter.1
where the time goes:
time: 156 us; the launch traced here: 155 us
  waiting for transfers between devices  68.8 us (44%)
  matrix products  32.1 us (21%)
  local copies, waits for them, and re-layouts  19.8 us (13%)
  loops' own time  16.6 us (11%)
  between operations  13.2 us (8%)
  other arithmetic  4.16 us (3%)
    all_gather x1, waiting for transfers between devices, body(): lax.all_gather(state, 'gx', axis=0, tiled=True)  43.2 us
    dot_general x8, matrix products, one_term(): jnp.einsum('jxa,japb->jxpb', matrix, source_block, preferred_element_type...  17.2 us
    another operation x1, loops' own time, apply_left(): return lax.map(one_term, (environment, charges))  16.6 us
    all_gather x1, waiting for transfers between devices, body(): applied = lax.all_gather(own_terms, 'gz', axis=0, tiled=True)  15.7 us
    reduce_scatter x1, waiting for transfers between devices, body(): lax.psum_scatter(partial_out, 'gz', scatter_dimension=2, tiled=True)  9.76 us
    while x2, local copies, waits for them, and re-layouts, apply_left(): return lax.map(one_term, (environment, charges))  8.37 us
    dot_general x1, matrix products, body(): jnp.einsum('uvpq,ujxqb->vjxpb', mpo_terms, applied, preferred_element_typ...  5.95 us
    dot_general x1, matrix products, body(): jnp.einsum('vjxpb,vbc->jxpc', mixed_terms, right_env, preferred_element_t...  5.57 us
  transfers between devices with their start and end apart: 3, of which 3 were waited for; matrix products, arithmetic and copies ran while one was open for 4% of the time, Pallas kernels for 0%

commit v1 on v0

v1 whole, which is shorter than its diff:
```python
import functools

import jax
import jax.numpy as jnp
from jax import lax
from jax.experimental import pallas as pl
from jax.experimental.pallas import tpu as pltpu
from jax.sharding import PartitionSpec as P

MESH = pl.DeviceIdType.MESH
TILE = 16
LANE = 128
SUB = 2


def kernel(
    n,
    phys,
    term_charge,
    charge_order,
    sector_dims,
    s_ref,
    m_ref,
    left_hbm,
    right_hbm,
    out_ref,
    g,
    left,
    right,
    m_all,
    big,
    arranged,
    mixed,
    total,
    send_sem,
    recv_sem,
    pass_send,
    pass_recv,
    misc_sem,
    keep_sem,
):
    i = lax.axis_index("gx")
    z = lax.axis_index("gz")
    other = 1 - z
    terms = left.shape[0]
    rows = left.shape[1]
    blocks = s_ref.shape[0]
    half = rows // 2
    piece = half // SUB
    own_terms = right_hbm.shape[0]
    own_phys = phys // 2
    has_up, has_down = i < n - 1, i > 0

    load_left = pltpu.make_async_copy(left_hbm, left, misc_sem.at[0])
    load_left.start()
    load_right = pltpu.make_async_copy(
        right_hbm, right.at[pl.ds(z * own_terms, own_terms)], misc_sem.at[1]
    )
    load_right.start()
    keep_m = pltpu.make_async_copy(m_ref, m_all.at[z], misc_sem.at[2])
    keep_m.start()
    keep_s = [
        pltpu.make_async_copy(s_ref.at[block], g[block].at[i], keep_sem.at[block])
        for block in range(blocks)
    ]
    for copy in keep_s:
        copy.start()

    barrier = pltpu.get_barrier_semaphore()

    @pl.when(has_up)
    def _():
        pl.semaphore_signal(barrier, inc=1, device_id={"gx": i + 1}, device_id_type=MESH)

    @pl.when(has_down)
    def _():
        pl.semaphore_signal(barrier, inc=1, device_id={"gx": i - 1}, device_id_type=MESH)

    pl.semaphore_signal(barrier, inc=1, device_id={"gz": other}, device_id_type=MESH)
    pl.semaphore_wait(barrier, 1 + has_up.astype(jnp.int32) + has_down.astype(jnp.int32))

    def span(sub):
        return pl.ds(pl.multiple_of(z * half + sub * piece, piece), piece)

    def hop(way, step, block, sub):
        source = i - step if way == 0 else i + step
        target = i + 1 if way == 0 else i - 1
        held = g[block].at[source, span(sub)]
        origin = s_ref.at[block, span(sub)] if step == 0 else held
        return pltpu.make_async_remote_copy(
            src_ref=origin,
            dst_ref=held,
            send_sem=send_sem.at[way, step, block, sub],
            recv_sem=recv_sem.at[way, step, block, sub],
            device_id={"gx": target},
            device_id_type=MESH,
        )

    def sends(way, step):
        if way == 0:
            return jnp.logical_and(has_up, i >= step)
        return jnp.logical_and(has_down, i + step <= n - 1)

    def receives(way, step):
        return i >= step + 1 if way == 0 else i + step + 1 <= n - 1

    def arrived(way, step, block, sub):
        source = i - 1 - step if way == 0 else i + 1 + step
        held = g[block].at[source, span(sub)]
        return pltpu.make_async_remote_copy(
            src_ref=held,
            dst_ref=held,
            send_sem=send_sem.at[way, step, block, sub],
            recv_sem=recv_sem.at[way, step, block, sub],
            device_id={"gx": i},
            device_id_type=MESH,
        )

    def across(way, step, block, sub, mine):
        source = i - 1 - step if way == 0 else i + 1 + step
        core = z if mine else other
        held = g[block].at[
            source, pl.ds(pl.multiple_of(core * half + sub * piece, piece), piece)
        ]
        return pltpu.make_async_remote_copy(
            src_ref=held,
            dst_ref=held,
            send_sem=pass_send.at[way, step, block, sub],
            recv_sem=pass_recv.at[way, step, block, sub],
            device_id={"gz": other},
            device_id_type=MESH,
        )

    def start_own(block):
        for sub in range(SUB):
            for way in (0, 1):

                @pl.when(sends(way, 0))
                def _():
                    hop(way, 0, block, sub).start()

    def event(block, step):
        for sub in range(SUB):
            for way in (0, 1):

                @pl.when(receives(way, step))
                def _():
                    arrived(way, step, block, sub).wait_recv()
                    if step + 1 < n - 1:

                        @pl.when(sends(way, step + 1))
                        def _():
                            hop(way, step + 1, block, sub).start()

                    across(way, step, block, sub, True).start()

    def finish(block):
        for step in range(n - 1):
            for sub in range(SUB):
                for way in (0, 1):

                    @pl.when(receives(way, step))
                    def _():
                        across(way, step, block, sub, False).wait_recv()

    start_own(0)
    give_m = pltpu.make_async_remote_copy(
        src_ref=m_ref,
        dst_ref=m_all.at[z],
        send_sem=misc_sem.at[4],
        recv_sem=misc_sem.at[5],
        device_id={"gz": other},
        device_id_type=MESH,
    )
    give_m.start()
    give_right = pltpu.make_async_remote_copy(
        src_ref=right_hbm,
        dst_ref=right.at[pl.ds(z * own_terms, own_terms)],
        send_sem=misc_sem.at[6],
        recv_sem=misc_sem.at[7],
        device_id={"gz": other},
        device_id_type=MESH,
    )
    give_right.start()

    for held in g:
        held[n] = jnp.zeros(held.shape[1:], held.dtype)

    keep_m.wait()
    give_m.wait()
    out_rows, in_rows = big.shape
    pairs = m_all.shape[1]
    r = lax.broadcasted_iota(jnp.int32, (out_rows, 2 * pairs), 0) // TILE
    k = lax.broadcasted_iota(jnp.int32, (out_rows, 2 * pairs), 1)
    v = r % terms
    p = r // terms + z * own_phys
    wanted = (v // own_terms) * pairs + p * own_terms + v % own_terms
    pick = (k == wanted).astype(jnp.bfloat16)
    coeffs = jnp.dot(
        pick,
        m_all[...].reshape(2 * pairs, m_all.shape[2]),
        preferred_element_type=jnp.float32,
    ).astype(jnp.bfloat16)
    width = m_all.shape[2]
    spread = (
        lax.broadcasted_iota(jnp.int32, (width, in_rows), 0)
        == lax.broadcasted_iota(jnp.int32, (width, in_rows), 1) // TILE
    ).astype(jnp.bfloat16)
    diagonal = (
        lax.broadcasted_iota(jnp.int32, (out_rows, in_rows), 0) % TILE
        == lax.broadcasted_iota(jnp.int32, (out_rows, in_rows), 1) % TILE
    )
    dense = jnp.dot(coeffs, spread, preferred_element_type=jnp.float32)
    big[...] = jnp.where(diagonal, dense, 0.0).astype(jnp.bfloat16)

    own_charge = charge_order[i]
    found = []
    for shift in range(3):
        place = jnp.int32(n)
        for sector in range(n):
            place = jnp.where(charge_order[sector] == own_charge + shift - 1, sector, place)
        found.append(place)

    def apply_left(block):
        def one_term(w, carry):
            charge = term_charge[w]
            source = jnp.where(charge == 0, found[0], jnp.where(charge == 1, found[1], found[2]))
            product = jnp.dot(
                left[w], g[block][source], preferred_element_type=jnp.float32
            ).astype(jnp.bfloat16)
            for group in range(rows // TILE):
                for q in range(phys):
                    at = pl.multiple_of(w * (phys * TILE) + q * TILE, TILE)
                    side = (group % 2) * LANE
                    arranged[group // 2, pl.ds(at, TILE), side : side + LANE] = product[
                        group * TILE : (group + 1) * TILE, q * LANE : (q + 1) * LANE
                    ]
            return carry

        lax.fori_loop(0, terms, one_term, 0)

    def mix():
        def one_pair(pair, carry):
            product = jnp.dot(
                big[...], arranged[pair], preferred_element_type=jnp.float32
            ).astype(jnp.bfloat16)
            for p in range(own_phys):
                for v in range(terms):
                    for side in range(2):
                        at = pl.multiple_of(p * rows + pair * 2 * TILE + side * TILE, TILE)
                        start = (p * terms + v) * TILE
                        mixed[pl.ds(at, TILE), v * LANE : (v + 1) * LANE] = product[
                            start : start + TILE, side * LANE : (side + 1) * LANE
                        ]
            return carry

        lax.fori_loop(0, arranged.shape[0], one_pair, 0)

    def apply_right(block):
        tiles = right[:, block * LANE : (block + 1) * LANE, :].reshape(
            terms * LANE, right.shape[2]
        )
        for p in range(own_phys):
            part = slice(p * rows, (p + 1) * rows)
            product = jnp.dot(mixed[part, :], tiles, preferred_element_type=jnp.float32)
            if block == 0:
                total[part, :] = product
            else:
                total[part, :] += product

    for step in range(n - 1):
        event(0, step)
    load_left.wait()
    for copy in keep_s:
        copy.wait()
    for block in range(blocks):
        more = block + 1 < blocks
        if more:
            start_own(block + 1)
        finish(block)
        apply_left(block)
        if more:
            event(block + 1, 0)
        mix()
        if block == 0:
            load_right.wait()
            give_right.wait()
        if more and n > 2:
            event(block + 1, 1)
        apply_right(block)
        if more:
            for step in range(2, n - 1):
                event(block + 1, step)

    used = sector_dims[i]
    mask = lax.broadcasted_iota(jnp.int32, (rows, total.shape[1]), 0) < used
    for p in range(own_phys):
        out_ref[p] = jnp.where(mask, total[p * rows : (p + 1) * rows, :], 0.0).astype(
            out_ref.dtype
        )

    for block in range(blocks):
        for step in range(n - 1):
            for sub in range(SUB):
                for way in (0, 1):

                    @pl.when(sends(way, step))
                    def _():
                        hop(way, step, block, sub).wait_send()

                    @pl.when(receives(way, step))
                    def _():
                        across(way, step, block, sub, True).wait_send()


def body(n, state, left_env, mpo_terms, right_env, term_charge, charge_order, sector_dims):
    _, rows, phys, cols = state.shape
    terms, own_terms = mpo_terms.shape[:2]
    blocks = cols // LANE
    own_phys = phys // 2
    arranged_state = (
        state.reshape(rows, phys, blocks, LANE)
        .transpose(2, 0, 1, 3)
        .reshape(blocks, rows, phys * LANE)
    )
    m_own = mpo_terms.transpose(2, 1, 0, 3).reshape(phys * own_terms, terms * phys)
    m_own = jnp.pad(m_own, ((0, 0), (0, -(terms * phys) % LANE)))
    smem = pl.BlockSpec(memory_space=pltpu.SMEM)
    vmem = pl.BlockSpec(memory_space=pltpu.VMEM)
    hbm = pl.BlockSpec(memory_space=pl.ANY)
    dma = pltpu.SemaphoreType.DMA
    steps = (2, n - 1, blocks, SUB)
    out = pl.pallas_call(
        functools.partial(kernel, n, phys),
        out_shape=jax.ShapeDtypeStruct((own_phys, rows, cols), jnp.bfloat16),
        in_specs=[smem, smem, smem, vmem, vmem, hbm, hbm],
        out_specs=vmem,
        scratch_shapes=[
            [pltpu.VMEM((n + 1, rows, phys * LANE), jnp.bfloat16) for _ in range(blocks)],
            pltpu.VMEM((terms, rows, rows), jnp.bfloat16),
            pltpu.VMEM((terms, cols, cols), jnp.bfloat16),
            pltpu.VMEM((2,) + m_own.shape, jnp.bfloat16),
            pltpu.VMEM((own_phys * terms * TILE, terms * phys * TILE), jnp.bfloat16),
            pltpu.VMEM((rows // TILE // 2, terms * phys * TILE, 2 * LANE), jnp.bfloat16),
            pltpu.VMEM((own_phys * rows, terms * LANE), jnp.bfloat16),
            pltpu.VMEM((own_phys * rows, cols), jnp.float32),
            dma(steps),
            dma(steps),
            dma(steps),
            dma(steps),
            dma((8,)),
            dma((blocks,)),
        ],
        compiler_params=pltpu.CompilerParams(
            collective_id=0, has_side_effects=True, vmem_limit_bytes=56 * 1024 * 1024
        ),
        name="two_site",
    )(
        term_charge,
        charge_order,
        sector_dims,
        arranged_state,
        m_own,
        left_env.reshape(left_env.shape[0], rows, rows),
        right_env,
    )
    return out.transpose(1, 0, 2)[None]


def solution(mesh):
    return jax.shard_map(
        functools.partial(body, mesh.shape["gx"]),
        mesh=mesh,
        in_specs=(
            P(("ga", "gx"), None, None, "gy"),
            P(None, ("ga", "gx"), None, None),
            P(None, "gz", None, None),
            P("gz", ("ga", "gy"), None),
            P(),
            P("ga"),
            P("ga"),
        ),
        out_specs=P(("ga", "gx"), None, "gz", "gy"),
        check_vma=False,
    )
```

time: 156 us -> 44.7 us (0.29)
  waiting for transfers between devices: 68.8 us -> 0 us
  Pallas kernels: 0 us -> 39.2 us
  matrix products: 32.1 us -> 0 us
  loops' own time: 16.6 us -> 0 us
  local copies, waits for them, and re-layouts: 19.8 us -> 5.23 us
  between operations: 13.2 us -> 0.03 us
  other arithmetic: 4.16 us -> 0 us
    all_gather x2 -> x0, waiting for transfers between devices: 58.9 us -> none  [the longest x1 43.2 us: body(): lax.all_gather(state, 'gx', axis=0, tiled=True)]
    pallas_call x0 -> x1, Pallas kernels: none -> 39.2 us  [body(): pl.pallas_call(functools.partial(kernel, n, phys), out_shape=jax.ShapeDty...]
    dot_general x11 -> x0, matrix products: 32.1 us -> none  [the longest x8 17.2 us: one_term(): jnp.einsum('jxa,japb->jxpb', matrix, source_block, preferred_element_type...]
    another operation x1 -> x0, loops' own time: 16.6 us -> none  [apply_left(): return lax.map(one_term, (environment, charges))]
    reduce_scatter x1 -> x0, waiting for transfers between devices: 9.76 us -> none  [body(): lax.psum_scatter(partial_out, 'gz', scatter_dimension=2, tiled=True)]
    while x2 -> x0, local copies, waits for them, and re-layouts: 8.37 us -> none  [apply_left(): return lax.map(one_term, (environment, charges))]
    dynamic_slice x12 -> x0, local copies, waits for them, and re-layouts: 7.97 us -> none  [the longest x8 5.28 us: apply_left(): return lax.map(one_term, (environment, charges))]
    reshape x0 -> x5, local copies, waits for them, and re-layouts: none -> 2.55 us  [the longest x2 1.38 us: body(): state.reshape(rows, phys, blocks, LANE).transpose(2, 0, 1, 3)]
  transfers between devices with their start and end apart: 3 -> 0, of which waited for: 3 -> 0; matrix products, arithmetic and copies ran while one was open for 4% -> 0% of each run, Pallas kernels for 0% -> 0%
where the time goes in v1:
time: 44.7 us; the launch traced here: 44.5 us
  Pallas kernels  39.2 us (88%)
  local copies, waits for them, and re-layouts  5.23 us (12%)
    pallas_call x1, Pallas kernels, body(): pl.pallas_call(functools.partial(kernel, n, phys), out_shape=jax.ShapeDty...  39.2 us
    broadcast_in_dim x1, local copies, waits for them, and re-layouts, body(): return out.transpose(1, 0, 2)[None]  1.92 us
    reshape x2, local copies, waits for them, and re-layouts, body(): state.reshape(rows, phys, blocks, LANE).transpose(2, 0, 1, 3)  1.38 us
    reshape x1, local copies, waits for them, and re-layouts, body(): arranged_state = state.reshape(rows, phys, blocks, LANE).transpose(2, 0,...  0.98 us

profile of v1, /device:TPU:1, one launch (start us, length us, event | category | flops | bytes accessed | tf_op | source)
XLA Modules:
  0.0 44.5 jit_solution(16380183772965488372)
XLA Ops:
  0.0 0.0 copy-start
  0.0 1.2 %reshape.12 = bf16[256,4,2,128]{3,2,1,0:T(2,128)(2,1)S(1)} reshape(bf16[1,256,4,256]{3,2,1,0:T(4,128)(2,1)} %param.7) | data formatting | bytes 1048576 | tf_op jit(solution)/shard_map/reshape | solution.py:322
  1.3 0.1 copy.16
  1.4 1.0 %reshape.13.s_ref = bf16[2,256,512]{2,1,0:T(8,128)(2,1)} reshape(bf16[2,256,4,128]{3,2,1,0:T(4,128)(2,1)S(1)} %bitcast.11) | data formatting | bytes 1048576 | tf_op jit(solution)/shard_map/reshape | solution.py:324
  2.4 0.0 copy-done
  2.4 0.1 copy.12
  2.5 0.1 reshape.14
  2.6 0.1 copy.13
  2.7 0.6 %pad.4.m_ref = bf16[32,128]{1,0:T(8,128)(2,1)} pad(bf16[32,64]{1,0:T(8,128)(2,1)S(1)} %copy.13, bf16[]{:T(256)} %constant.2.clone.1), padding=0_0x0_64 | pad | bytes 12290 | tf_op jit(solution)/shard_map/jit(_pad)/pad | solution.py:327
  3.3 39.2 %two_site.1 = bf16[2,256,256]{2,1,0:T(8,128)(2,1)} custom-call(s32[16]{0:T(128)} %term_charge.1, s32[4]{0:T(128)} %charge_order.1, s32[4]{0:T(128)} %sector_dims.1, bf16[2,256,512]{2,1,0:T(8,128)(2,1)} %reshape.13.s_ref, bf16[32,128]{1,0:T(8,128)(2,1)} %pad.4.m_ref, bf16[16,256,256]{2,1,0:T(8,128)(2,1)} %bitcast.10, bf16[8,256,256]{2,1,0:T(8,128)(2,1)} %right_hbm.1), custom_call_target="tpu_custom_call" | custom-call | tf_op jit(solution)/shard_map/two_site/pallas_call | solution.py:333
  42.6 1.9 %copy.14 = bf16[1,256,2,256]{3,2,1,0:T(2,128)(2,1)} copy(bf16[1,256,2,256]{3,1,2,0:T(8,128)(2,1)} %bitcast.12) | data formatting | bytes 524288 | tf_op jit(solution)/shard_map/broadcast_in_dim | solution.py:367
Async XLA Ops:
  0.0 2.4 %copy-start = (bf16[16,8,4,4]{0,3,2,1:T(4,128)(2,1)S(1)}, bf16[16,8,4,4]{0,3,2,1:T(4,128)(2,1)}, u32[]{:S(2)}) copy-start(bf16[16,8,4,4]{0,3,2,1:T(4,128)(2,1)} %param.9) | copy-start | bytes 12292

commit v2 on v1

--- a/solution.py
+++ b/solution.py
@@ -44,7 +44,7 @@
     other = 1 - z
     terms = left.shape[0]
     rows = left.shape[1]
-    blocks = s_ref.shape[0]
+    blocks = len(g)
     half = rows // 2
     piece = half // SUB
     own_terms = right_hbm.shape[0]
@@ -60,7 +60,11 @@
     keep_m = pltpu.make_async_copy(m_ref, m_all.at[z], misc_sem.at[2])
     keep_m.start()
     keep_s = [
-        pltpu.make_async_copy(s_ref.at[block], g[block].at[i], keep_sem.at[block])
+        pltpu.make_async_copy(
+            s_ref.at[:, :, block * LANE : (block + 1) * LANE],
+            g[block].at[i],
+            keep_sem.at[block],
+        )
         for block in range(blocks)
     ]
     for copy in keep_s:
@@ -85,8 +89,8 @@
     def hop(way, step, block, sub):
         source = i - step if way == 0 else i + step
         target = i + 1 if way == 0 else i - 1
-        held = g[block].at[source, span(sub)]
-        origin = s_ref.at[block, span(sub)] if step == 0 else held
+        held = g[block].at[source, :, span(sub)]
+        origin = s_ref.at[:, span(sub), block * LANE : (block + 1) * LANE] if step == 0 else held
         return pltpu.make_async_remote_copy(
             src_ref=origin,
             dst_ref=held,
@@ -106,7 +110,7 @@
 
     def arrived(way, step, block, sub):
         source = i - 1 - step if way == 0 else i + 1 + step
-        held = g[block].at[source, span(sub)]
+        held = g[block].at[source, :, span(sub)]
         return pltpu.make_async_remote_copy(
             src_ref=held,
             dst_ref=held,
@@ -120,7 +124,7 @@
         source = i - 1 - step if way == 0 else i + 1 + step
         core = z if mine else other
         held = g[block].at[
-            source, pl.ds(pl.multiple_of(core * half + sub * piece, piece), piece)
+            source, :, pl.ds(pl.multiple_of(core * half + sub * piece, piece), piece)
         ]
         return pltpu.make_async_remote_copy(
             src_ref=held,
@@ -190,8 +194,9 @@
     give_m.wait()
     out_rows, in_rows = big.shape
     pairs = m_all.shape[1]
-    r = lax.broadcasted_iota(jnp.int32, (out_rows, 2 * pairs), 0) // TILE
-    k = lax.broadcasted_iota(jnp.int32, (out_rows, 2 * pairs), 1)
+    kept = own_phys * terms
+    r = lax.broadcasted_iota(jnp.int32, (kept, 2 * pairs), 0)
+    k = lax.broadcasted_iota(jnp.int32, (kept, 2 * pairs), 1)
     v = r % terms
     p = r // terms + z * own_phys
     wanted = (v // own_terms) * pairs + p * own_terms + v % own_terms
@@ -207,11 +212,14 @@
         == lax.broadcasted_iota(jnp.int32, (width, in_rows), 1) // TILE
     ).astype(jnp.bfloat16)
     diagonal = (
-        lax.broadcasted_iota(jnp.int32, (out_rows, in_rows), 0) % TILE
-        == lax.broadcasted_iota(jnp.int32, (out_rows, in_rows), 1) % TILE
+        lax.broadcasted_iota(jnp.int32, (TILE, in_rows), 0)
+        == lax.broadcasted_iota(jnp.int32, (TILE, in_rows), 1) % TILE
     )
     dense = jnp.dot(coeffs, spread, preferred_element_type=jnp.float32)
-    big[...] = jnp.where(diagonal, dense, 0.0).astype(jnp.bfloat16)
+    for row in range(kept):
+        big[row * TILE : (row + 1) * TILE, :] = jnp.where(
+            diagonal, dense[row : row + 1, :], 0.0
+        ).astype(jnp.bfloat16)
 
     own_charge = charge_order[i]
     found = []
@@ -225,8 +233,11 @@
         def one_term(w, carry):
             charge = term_charge[w]
             source = jnp.where(charge == 0, found[0], jnp.where(charge == 1, found[1], found[2]))
+            taken = g[block][source]
             product = jnp.dot(
-                left[w], g[block][source], preferred_element_type=jnp.float32
+                left[w],
+                jnp.concatenate([taken[q] for q in range(phys)], axis=1),
+                preferred_element_type=jnp.float32,
             ).astype(jnp.bfloat16)
             for group in range(rows // TILE):
                 for q in range(phys):
@@ -237,7 +248,7 @@
                     ]
             return carry
 
-        lax.fori_loop(0, terms, one_term, 0)
+        lax.fori_loop(0, terms, one_term, 0, unroll=8)
 
     def mix():
         def one_pair(pair, carry):
@@ -254,7 +265,7 @@
                         ]
             return carry
 
-        lax.fori_loop(0, arranged.shape[0], one_pair, 0)
+        lax.fori_loop(0, arranged.shape[0], one_pair, 0, unroll=4)
 
     def apply_right(block):
         tiles = right[:, block * LANE : (block + 1) * LANE, :].reshape(
@@ -318,13 +329,8 @@
     terms, own_terms = mpo_terms.shape[:2]
     blocks = cols // LANE
     own_phys = phys // 2
-    arranged_state = (
-        state.reshape(rows, phys, blocks, LANE)
-        .transpose(2, 0, 1, 3)
-        .reshape(blocks, rows, phys * LANE)
-    )
+    arranged_state = state.reshape(rows, phys, cols).transpose(1, 0, 2)
     m_own = mpo_terms.transpose(2, 1, 0, 3).reshape(phys * own_terms, terms * phys)
-    m_own = jnp.pad(m_own, ((0, 0), (0, -(terms * phys) % LANE)))
     smem = pl.BlockSpec(memory_space=pltpu.SMEM)
     vmem = pl.BlockSpec(memory_space=pltpu.VMEM)
     hbm = pl.BlockSpec(memory_space=pl.ANY)
@@ -336,7 +342,7 @@
         in_specs=[smem, smem, smem, vmem, vmem, hbm, hbm],
         out_specs=vmem,
         scratch_shapes=[
-            [pltpu.VMEM((n + 1, rows, phys * LANE), jnp.bfloat16) for _ in range(blocks)],
+            [pltpu.VMEM((n + 1, phys, rows, LANE), jnp.bfloat16) for _ in range(blocks)],
             pltpu.VMEM((terms, rows, rows), jnp.bfloat16),
             pltpu.VMEM((terms, cols, cols), jnp.bfloat16),
             pltpu.VMEM((2,) + m_own.shape, jnp.bfloat16),

time: 44.7 us -> 40.9 us (0.915)
  Pallas kernels: 39.2 us -> 35.1 us
    pallas_call x1, Pallas kernels: 39.2 us -> 35.1 us  [body(): pl.pallas_call(functools.partial(kernel, n, phys), out_shape=jax.ShapeDty...]
    reshape x3 -> x0, local copies, waits for them, and re-layouts: 2.37 us -> none  [the longest x2 1.38 us: body(): state.reshape(rows, phys, blocks, LANE).transpose(2, 0, 1, 3)]
    unnamed x2 -> x1, local copies, waits for them, and re-layouts: 0.01 us -> 1.9 us
    transpose x1, local copies, waits for them, and re-layouts: 0.14 us -> 0.88 us  [body(): mpo_terms.transpose(2, 1, 0, 3).reshape(phys * own_terms, terms * phys)]
    pad x1 -> x0, local copies, waits for them, and re-layouts: 0.62 us -> none  [body(): m_own = jnp.pad(m_own, ((0, 0), (0, -(terms * phys) % LANE)))]
    reshape x2, local copies, waits for them, and re-layouts: 0.18 us -> 0.79 us  [body(): mpo_terms.transpose(2, 1, 0, 3).reshape(phys * own_terms, terms * phys)]
where the time goes in v2:
time: 40.9 us; the launch traced here: 40.6 us
  Pallas kernels  35.1 us (86%)
  local copies, waits for them, and re-layouts  5.49 us (13%)
    pallas_call x1, Pallas kernels, body(): pl.pallas_call(functools.partial(kernel, n, phys), out_shape=jax.ShapeDty...  35.1 us
    broadcast_in_dim x1, local copies, waits for them, and re-layouts, body(): return out.transpose(1, 0, 2)[None]  1.92 us
    unnamed x1, local copies, waits for them, and re-layouts  1.9 us
    transpose x1, local copies, waits for them, and re-layouts, body(): mpo_terms.transpose(2, 1, 0, 3).reshape(phys * own_terms, terms * phys)  0.88 us

profile of v2, /device:TPU:1, one launch (start us, length us, event | category | flops | bytes accessed | tf_op | source)
XLA Modules:
  0.0 40.6 jit_solution(12011943583087893179)
XLA Ops:
  0.0 0.9 %copy.12 = bf16[4,8,16,4]{1,0,3,2:T(4,128)(2,1)S(1)} copy(bf16[4,8,16,4]{2,3,0,1:T(4,128)(2,1)} %bitcast.15) | data formatting | bytes 8192 | tf_op jit(solution)/shard_map/transpose | solution.py:333
  0.9 0.1 reshape.10
  1.0 0.7 %copy.13.m_ref = bf16[32,64]{1,0:T(8,128)(2,1)} copy(bf16[32,64]{0,1:T(8,128)(2,1)S(1)} %reshape.10) | data formatting | bytes 8192 | tf_op jit(solution)/shard_map/reshape | solution.py:333
  1.7 1.9 %copy.16 = bf16[1,256,4,256]{3,1,2,0:T(8,128)(2,1)} copy(bf16[1,256,4,256]{3,2,1,0:T(4,128)(2,1)} %param.7) | data formatting | bytes 1048576 | tf_op args[0]
  3.6 35.1 %two_site.1 = bf16[2,256,256]{2,1,0:T(8,128)(2,1)} custom-call(s32[16]{0:T(128)} %term_charge.1, s32[4]{0:T(128)} %charge_order.1, s32[4]{0:T(128)} %sector_dims.1, bf16[4,256,256]{2,1,0:T(8,128)(2,1)} %bitcast.13, bf16[32,64]{1,0:T(8,128)(2,1)} %copy.13.m_ref, bf16[16,256,256]{2,1,0:T(8,128)(2,1)} %bitcast.12, bf16[8,256,256]{2,1,0:T(8,128)(2,1)} %right_hbm.1), custom_call_target="tpu_custom_call" | custom-call | tf_op jit(solution)/shard_map/two_site/pallas_call | solution.py:339
  38.7 1.9 %copy.14 = bf16[1,256,2,256]{3,2,1,0:T(2,128)(2,1)} copy(bf16[1,256,2,256]{3,1,2,0:T(8,128)(2,1)} %bitcast.14) | data formatting | bytes 524288 | tf_op jit(solution)/shard_map/broadcast_in_dim | solution.py:373

commit v3 on v2

--- a/solution.py
+++ b/solution.py
@@ -28,6 +28,7 @@
     left,
     right,
     m_all,
+    coeffs,
     big,
     arranged,
     mixed,
@@ -38,6 +39,11 @@
     pass_recv,
     misc_sem,
     keep_sem,
+    stage,
+    pick_send,
+    pick_recv,
+    pick_pass_send,
+    pick_pass_recv,
 ):
     i = lax.axis_index("gx")
     z = lax.axis_index("gz")
@@ -100,13 +106,17 @@
             device_id_type=MESH,
         )
 
+    picky = 1 if n >= 4 else 0
+
     def sends(way, step):
         if way == 0:
-            return jnp.logical_and(has_up, i >= step)
-        return jnp.logical_and(has_down, i + step <= n - 1)
+            return jnp.logical_and(i < n - 1 - picky, i >= step)
+        return jnp.logical_and(i > picky, i + step <= n - 1)
 
     def receives(way, step):
-        return i >= step + 1 if way == 0 else i + step + 1 <= n - 1
+        if way == 0:
+            return jnp.logical_and(i >= step + 1, i <= n - 1 - picky)
+        return jnp.logical_and(i + step + 1 <= n - 1, i >= picky)
 
     def arrived(way, step, block, sub):
         source = i - 1 - step if way == 0 else i + 1 + step
@@ -135,6 +145,86 @@
             device_id_type=MESH,
         )
 
+    def find(sector_charge, shift):
+        place = jnp.int32(n)
+        for sector in range(n):
+            place = jnp.where(charge_order[sector] == sector_charge + shift - 1, sector, place)
+        return place
+
+    def choice(way):
+        end_charge = charge_order[n - 1 if way == 0 else 0]
+        first, second = find(end_charge, 0), find(end_charge, 2)
+        if way == 0:
+            first = jnp.where(first < n, n - 1 - first, n)
+            second = jnp.where(second < n, n - 1 - second, n)
+        near, far = jnp.minimum(first, second), jnp.maximum(first, second)
+        return (
+            jnp.where(near < n - 1, near, 1),
+            jnp.where(far < n, far, near),
+            first,
+            second,
+        )
+
+    found = [find(charge_order[i], shift) for shift in range(3)]
+    choices = [choice(way) for way in (0, 1)] if picky else []
+    for way in range(len(choices)):
+        early, _, first, second = choices[way]
+        end = n - 1 if way == 0 else 0
+        for shift, sought in ((0, first), (2, second)):
+            one, two = (n - 2, n - 3) if way == 0 else (1, 2)
+            place = jnp.where(sought == n, n, jnp.where(sought == early, one, two))
+            found[shift] = jnp.where(i == end, place, found[shift])
+
+    half_rows = pl.ds(pl.multiple_of(z * half, half), half)
+    other_rows = pl.ds(pl.multiple_of(other * half, half), half)
+
+    def picked(way, which, block, passing, mine=True):
+        slot = (n - 2 - which) if way == 0 else 1 + which
+        held = g[block].at[slot, :, half_rows if mine else other_rows]
+        return pltpu.make_async_remote_copy(
+            src_ref=held if passing else stage.at[which, block],
+            dst_ref=held,
+            send_sem=(pick_pass_send if passing else pick_send).at[way, which, block],
+            recv_sem=(pick_pass_recv if passing else pick_recv).at[way, which, block],
+            device_id={"gz": other} if passing else {"gx": n - 1 if way == 0 else 0},
+            device_id_type=MESH,
+        )
+
+    def pick(block, which):
+        for way in range(len(choices)):
+
+            @pl.when(i == (n - 2 if way == 0 else 1))
+            def _():
+                value = s_ref[:, half_rows, block * LANE : (block + 1) * LANE]
+                for place in range(2, n - 1 + which):
+                    slot = n - 1 - place if way == 0 else place
+                    value = jnp.where(
+                        choices[way][which] == place, g[block][slot, :, half_rows], value
+                    )
+                stage[which, block] = value
+                picked(way, which, block, False).start()
+
+    def take(block, which):
+        for way in range(len(choices)):
+
+            @pl.when(i == (n - 1 if way == 0 else 0))
+            def _():
+                picked(way, which, block, False).wait_recv()
+                picked(way, which, block, True).start()
+
+    def settle():
+        for block in range(blocks):
+            for which in range(2):
+                for way in range(len(choices)):
+
+                    @pl.when(i == (n - 2 if way == 0 else 1))
+                    def _():
+                        picked(way, which, block, False).wait_send()
+
+                    @pl.when(i == (n - 1 if way == 0 else 0))
+                    def _():
+                        picked(way, which, block, True).wait_send()
+
     def start_own(block):
         for sub in range(SUB):
             for way in (0, 1):
@@ -158,6 +248,14 @@
 
                     across(way, step, block, sub, True).start()
 
+    def flow(block, step):
+        event(block, step)
+        if picky and step == n - 4:
+            pick(block, 0)
+        if picky and step == n - 3:
+            pick(block, 1)
+            take(block, 0)
+
     def finish(block):
         for step in range(n - 1):
             for sub in range(SUB):
@@ -166,6 +264,12 @@
                     @pl.when(receives(way, step))
                     def _():
                         across(way, step, block, sub, False).wait_recv()
+        for way in range(len(choices)):
+
+            @pl.when(i == (n - 1 if way == 0 else 0))
+            def _():
+                for which in range(2):
+                    picked(way, which, block, True, False).wait_recv()
 
     start_own(0)
     give_m = pltpu.make_async_remote_copy(
@@ -192,42 +296,28 @@
 
     keep_m.wait()
     give_m.wait()
-    out_rows, in_rows = big.shape
-    pairs = m_all.shape[1]
     kept = own_phys * terms
-    r = lax.broadcasted_iota(jnp.int32, (kept, 2 * pairs), 0)
-    k = lax.broadcasted_iota(jnp.int32, (kept, 2 * pairs), 1)
-    v = r % terms
-    p = r // terms + z * own_phys
-    wanted = (v // own_terms) * pairs + p * own_terms + v % own_terms
-    pick = (k == wanted).astype(jnp.bfloat16)
-    coeffs = jnp.dot(
-        pick,
-        m_all[...].reshape(2 * pairs, m_all.shape[2]),
-        preferred_element_type=jnp.float32,
-    ).astype(jnp.bfloat16)
-    width = m_all.shape[2]
+    width = terms * TILE
     spread = (
-        lax.broadcasted_iota(jnp.int32, (width, in_rows), 0)
-        == lax.broadcasted_iota(jnp.int32, (width, in_rows), 1) // TILE
+        lax.broadcasted_iota(jnp.int32, (terms, width), 0)
+        == lax.broadcasted_iota(jnp.int32, (terms, width), 1) // TILE
     ).astype(jnp.bfloat16)
     diagonal = (
-        lax.broadcasted_iota(jnp.int32, (TILE, in_rows), 0)
-        == lax.broadcasted_iota(jnp.int32, (TILE, in_rows), 1) % TILE
-    )
-    dense = jnp.dot(coeffs, spread, preferred_element_type=jnp.float32)
+        lax.broadcasted_iota(jnp.int32, (TILE, width), 0)
+        == lax.broadcasted_iota(jnp.int32, (TILE, width), 1) % TILE
+    )
+    entries = m_all.shape[1]
+    coeffs[...] = jnp.dot(
+        m_all[...].reshape(2 * entries, terms), spread, preferred_element_type=jnp.float32
+    )
     for row in range(kept):
-        big[row * TILE : (row + 1) * TILE, :] = jnp.where(
-            diagonal, dense[row : row + 1, :], 0.0
-        ).astype(jnp.bfloat16)
-
-    own_charge = charge_order[i]
-    found = []
-    for shift in range(3):
-        place = jnp.int32(n)
-        for sector in range(n):
-            place = jnp.where(charge_order[sector] == own_charge + shift - 1, sector, place)
-        found.append(place)
+        v = row % terms
+        p = row // terms + z * own_phys
+        for q in range(phys):
+            at = (v // own_terms) * entries + ((v % own_terms) * phys + p) * phys + q
+            big[row * TILE : (row + 1) * TILE, q * width : (q + 1) * width] = jnp.where(
+                diagonal, coeffs[pl.ds(at, 1), :], 0.0
+            ).astype(jnp.bfloat16)
 
     def apply_left(block):
         def one_term(w, carry):
@@ -241,7 +331,7 @@
             ).astype(jnp.bfloat16)
             for group in range(rows // TILE):
                 for q in range(phys):
-                    at = pl.multiple_of(w * (phys * TILE) + q * TILE, TILE)
+                    at = pl.multiple_of(w * TILE + q * (terms * TILE), TILE)
                     side = (group % 2) * LANE
                     arranged[group // 2, pl.ds(at, TILE), side : side + LANE] = product[
                         group * TILE : (group + 1) * TILE, q * LANE : (q + 1) * LANE
@@ -280,7 +370,8 @@
                 total[part, :] += product
 
     for step in range(n - 1):
-        event(0, step)
+        flow(0, step)
+    take(0, 1)
     load_left.wait()
     for copy in keep_s:
         copy.wait()
@@ -291,18 +382,20 @@
         finish(block)
         apply_left(block)
         if more:
-            event(block + 1, 0)
+            flow(block + 1, 0)
         mix()
         if block == 0:
             load_right.wait()
             give_right.wait()
         if more and n > 2:
-            event(block + 1, 1)
+            flow(block + 1, 1)
         apply_right(block)
         if more:
             for step in range(2, n - 1):
-                event(block + 1, step)
-
+                flow(block + 1, step)
+            take(block + 1, 1)
+
+    settle()
     used = sector_dims[i]
     mask = lax.broadcasted_iota(jnp.int32, (rows, total.shape[1]), 0) < used
     for p in range(own_phys):
@@ -330,7 +423,7 @@
     blocks = cols // LANE
     own_phys = phys // 2
     arranged_state = state.reshape(rows, phys, cols).transpose(1, 0, 2)
-    m_own = mpo_terms.transpose(2, 1, 0, 3).reshape(phys * own_terms, terms * phys)
+    m_own = mpo_terms.transpose(1, 2, 3, 0).reshape(own_terms * phys * phys, terms)
     smem = pl.BlockSpec(memory_space=pltpu.SMEM)
     vmem = pl.BlockSpec(memory_space=pltpu.VMEM)
     hbm = pl.BlockSpec(memory_space=pl.ANY)
@@ -346,6 +439,7 @@
             pltpu.VMEM((terms, rows, rows), jnp.bfloat16),
             pltpu.VMEM((terms, cols, cols), jnp.bfloat16),
             pltpu.VMEM((2,) + m_own.shape, jnp.bfloat16),
+            pltpu.VMEM((2 * m_own.shape[0], terms * TILE), jnp.float32),
             pltpu.VMEM((own_phys * terms * TILE, terms * phys * TILE), jnp.bfloat16),
             pltpu.VMEM((rows // TILE // 2, terms * phys * TILE, 2 * LANE), jnp.bfloat16),
             pltpu.VMEM((own_phys * rows, terms * LANE), jnp.bfloat16),
@@ -356,6 +450,11 @@
             dma(steps),
             dma((8,)),
             dma((blocks,)),
+            pltpu.VMEM((2, blocks, phys, rows // 2, LANE), jnp.bfloat16),
+            dma((2, 2, blocks)),
+            dma((2, 2, blocks)),
+            dma((2, 2, blocks)),
+            dma((2, 2, blocks)),
         ],
         compiler_params=pltpu.CompilerParams(
             collective_id=0, has_side_effects=True, vmem_limit_bytes=56 * 1024 * 1024

time: 40.9 us -> 39.8 us (0.973)
  local copies, waits for them, and re-layouts: 5.49 us -> 3.82 us
  Pallas kernels: 35.1 us -> 35.8 us
    transpose x1 -> x0, local copies, waits for them, and re-layouts: 0.88 us -> none  [body(): mpo_terms.transpose(2, 1, 0, 3).reshape(phys * own_terms, terms * phys)]
    reshape x2 -> x0, local copies, waits for them, and re-layouts: 0.79 us -> none  [body(): mpo_terms.transpose(2, 1, 0, 3).reshape(phys * own_terms, terms * phys)]
    pallas_call x1, Pallas kernels: 35.1 us -> 35.8 us  [body(): pl.pallas_call(functools.partial(kernel, n, phys), out_shape=jax.ShapeDty...]
where the time goes in v3:
time: 39.8 us; the launch traced here: 39.6 us
  Pallas kernels  35.8 us (90%)
  local copies, waits for them, and re-layouts  3.82 us (10%)
    pallas_call x1, Pallas kernels, body(): pl.pallas_call(functools.partial(kernel, n, phys), out_shape=jax.ShapeDty...  35.8 us
    broadcast_in_dim x1, local copies, waits for them, and re-layouts, body(): return out.transpose(1, 0, 2)[None]  1.92 us
    unnamed x1, local copies, waits for them, and re-layouts  1.9 us

profile of v3, /device:TPU:1, one launch (start us, length us, event | category | flops | bytes accessed | tf_op | source)
XLA Modules:
  0.0 39.6 jit_solution(265947844191955492)
XLA Ops:
  0.0 1.9 %copy.11 = bf16[1,256,4,256]{3,1,2,0:T(8,128)(2,1)} copy(bf16[1,256,4,256]{3,2,1,0:T(4,128)(2,1)} %param.7) | data formatting | bytes 1048576 | tf_op args[0]
  1.9 35.8 %two_site.1 = bf16[2,256,256]{2,1,0:T(8,128)(2,1)} custom-call(s32[16]{0:T(128)} %term_charge.1, s32[4]{0:T(128)} %charge_order.1, s32[4]{0:T(128)} %sector_dims.1, bf16[4,256,256]{2,1,0:T(8,128)(2,1)} %bitcast.13, bf16[128,16]{1,0:T(8,128)(2,1)} %bitcast.15, bf16[16,256,256]{2,1,0:T(8,128)(2,1)} %bitcast.12, bf16[8,256,256]{2,1,0:T(8,128)(2,1)} %right_hbm.1), custom_call_target="tpu_custom_call" | custom-call | tf_op jit(solution)/shard_map/two_site/pallas_call | solution.py:432
  37.7 1.9 %copy.9 = bf16[1,256,2,256]{3,2,1,0:T(2,128)(2,1)} copy(bf16[1,256,2,256]{3,1,2,0:T(8,128)(2,1)} %bitcast.14) | data formatting | bytes 524288 | tf_op jit(solution)/shard_map/broadcast_in_dim | solution.py:472
